TPU v7x, 32 devices: a whole 2x2x4 slice. The times are simulated.
32 devices in a mesh: dp: 2 (over core), tensor: 16 (over z, y, x).
Axes of the slice: x: 2, y: 2, z: 4, core: 2. Of those that a mesh axis runs over, the one named last changes fastest.
Arguments:
- gradient: float32 [2, 8192, 512], P('dp', 'tensor'), may hold values from -80 to 80
Outputs:
- update: bfloat16 [2, 8192, 512], P(None, 'tensor')
All inputs are finite; a program needn't handle non-finite values.
Results may differ from a plain program's by a relative error of at most 0.001.
Values may be sent and summed in bfloat16 or wider, within the bound.
No kernel may reach another device: no remote copies, remote signals or barrier semaphores. Data moves between devices by JAX's collectives and lax.ppermute only.
A program may use at most 64 MiB of HBM per device.

v0:
```python
import math
import jax
import jax.numpy as jnp
from jax import lax
from jax.sharding import PartitionSpec as P

FEATURES = 8192
OUTPUTS = 512
ITERS = 3
linear_term = 3.4445
cubic_term = -4.775
quintic_term = 2.0315
norm_floor = 1e-07
update_gain = 0.2


def multiply(first_factor, second_factor):
    return jnp.einsum("mrs,mst->mrt", first_factor, second_factor, precision=lax.Precision.HIGHEST)


def local_gram(gradient):
    return jnp.einsum("mfr,mfs->mrs", gradient, gradient, precision=lax.Precision.HIGHEST)


def reduce_gram(partial_gram):
    return lax.psum(partial_gram, "tensor")


def replicated_total(gram_matrix):
    order = gram_matrix.shape[2]
    identity = jnp.eye(order, dtype=jnp.float32)[None]
    running = identity
    for turn_index in range(ITERS):
        squared = multiply(gram_matrix, gram_matrix)
        polynomial = linear_term * identity + cubic_term * gram_matrix + quintic_term * squared
        if turn_index == 0:
            running = polynomial
        else:
            running = multiply(running, polynomial)
        if turn_index + 1 < ITERS:
            gram_matrix = multiply(multiply(polynomial, gram_matrix), polynomial)
    return running


def on_device(gradient):
    summed = reduce_gram(local_gram(gradient))
    squared_norm = jnp.trace(summed, axis1=1, axis2=2)
    divisor = jnp.sqrt(squared_norm) + norm_floor
    gram_matrix = summed / (divisor * divisor)[:, None, None]
    polished = jnp.einsum(
        "mfr,mrs->mfs", gradient, replicated_total(gram_matrix), precision=lax.Precision.HIGHEST
    )
    factor = update_gain * math.sqrt(max(FEATURES, OUTPUTS)) / divisor
    update = (factor[:, None, None] * polished).astype(jnp.bfloat16)
    return lax.all_gather(update, "dp", axis=0, tiled=True)


def solution(mesh):
    placed = (P("dp", "tensor", None),)
    return jax.shard_map(
        on_device, mesh=mesh, in_specs=placed, out_specs=P(None, "tensor", None), check_vma=False
    )
```

profile of v0, /device:TPU:0, one launch (start us, length us, event | category | flops | bytes accessed | tf_op | source)
XLA Modules:
  0.0 171.5 jit_solution(2133667007509548431)
XLA Ops:
  6.5 0.0 copy-start
  6.5 0.0 all-reduce.2.cloned.1.call-start
  6.5 1.2 copy-done
  7.8 2.8 %convolution_bitcast_fusion = f32[1,512,512]{2,1,0:T(8,128)} fusion(f32[1,512,512]{2,1,0:T(8,128)S(1)} %copy-done), kind=kOutput, calls=%fused_computation.9 | convolution fusion | flops 1610612736 | bytes 2097152 | tf_op jit(solution)/shard_map/mfr,mfs->mrs/dot_general | solution.py:22
  10.6 0.0 all-reduce.2.cloned.1.call-update
  10.6 0.0 all-gather.3.cloned.1.call-start
  10.7 117.1 %all-reduce.2.cloned.1.call-done = f32[1,512,512]{2,1,0:T(8,128)} async-done(((f32[1,512,512]{2,1,0:T(8,128)}), f32[1,512,512]{2,1,0:T(8,128)}) %all-reduce.2.cloned.1.call-update) | async-done | bytes 1048592 | tf_op jit(solution)/shard_map/psum | solution.py:26
  127.8 0.0 copy-start.1
  127.8 2.0 %select_reduce_fusion = f32[]{:T(128)} fusion(f32[1,512,512]{2,1,0:T(8,128)} %all-reduce.2.cloned.1.call-done), kind=kLoop, calls=%fused_computation.20 | loop fusion | flops 786431 | bytes 1048580 | tf_op jit(solution)/shard_map/jit(trace)/reduce_sum | solution.py:47
  130.5 0.0 copy-done.1
  130.5 1.9 %fusion.4 = f32[512,512]{1,0:T(8,128)S(1)} fusion(f32[1,512,512]{2,1,0:T(8,128)S(1)} %copy-done.1, f32[]{:T(128)S(6)} %mul.52), kind=kOutput, calls=%fused_computation.11 | convolution fusion | flops 1612709888 | bytes 2097156 | tf_op jit(solution)/shard_map/mrs,mst->mrt/dot_general | solution.py:18
  132.5 1.9 %fusion.7 = f32[512,512]{1,0:T(8,128)S(1)} fusion(f32[512,512]{1,0:T(8,128)S(1)} %fusion.4, f32[1,512,512]{2,1,0:T(8,128)S(1)} %copy-done.1, f32[]{:T(128)S(6)} %mul.52), kind=kOutput, calls=%fused_computation.14 | convolution fusion | flops 1610874880 | bytes 3145732 | tf_op jit(solution)/shard_map/mrs,mst->mrt/dot_general | solution.py:18
  134.3 1.8 %fusion.12 = f32[512,512]{1,0:T(8,128)S(1)} fusion(f32[512,512]{1,0:T(8,128)S(1)} %fusion.7, f32[512,512]{1,0:T(8,128)S(1)} %fusion.4), kind=kOutput, calls=%fused_computation.23 | convolution fusion | flops 1610612736 | bytes 3145728 | tf_op jit(solution)/shard_map/mrs,mst->mrt/dot_general | solution.py:18
  136.2 1.9 %fusion.1 = f32[512,512]{1,0:T(8,128)S(1)} fusion(f32[512,512]{1,0:T(8,128)S(1)} %fusion.12), kind=kOutput, calls=%fused_computation.6 | convolution fusion | flops 1612185600 | bytes 2097152 | tf_op jit(solution)/shard_map/mrs,mst->mrt/dot_general | solution.py:18
  138.1 2.8 %fusion.14 = f32[512,512]{1,0:T(8,128)} fusion(f32[512,512]{1,0:T(8,128)S(1)} %fusion.1, f32[512,512]{1,0:T(8,128)S(1)} %fusion.12), kind=kOutput, calls=%fused_computation.25 | convolution fusion | flops 1610612736 | bytes 3145728 | tf_op jit(solution)/shard_map/mrs,mst->mrt/dot_general | solution.py:18
  140.9 1.8 %fusion.13 = f32[512,512]{1,0:T(8,128)S(1)} fusion(f32[512,512]{1,0:T(8,128)S(1)} %fusion.4, f32[512,512]{1,0:T(8,128)S(1)} %fusion.1), kind=kOutput, calls=%fused_computation.24 | convolution fusion | flops 1610612736 | bytes 3145728 | tf_op jit(solution)/shard_map/mrs,mst->mrt/dot_general | solution.py:18
  142.8 3.2 %fusion.15 = f32[512,512]{1,0:T(8,128)S(1)} fusion(f32[512,512]{1,0:T(8,128)} %fusion.14, f32[512,512]{1,0:T(8,128)S(1)} %fusion.1), kind=kOutput, calls=%fused_computation.26 | convolution fusion | flops 1610612736 | bytes 3145728 | tf_op jit(solution)/shard_map/mrs,mst->mrt/dot_general | solution.py:18
  146.1 1.9 %fusion = f32[512,512]{1,0:T(8,128)S(1)} fusion(f32[512,512]{1,0:T(8,128)S(1)} %fusion.15), kind=kOutput, calls=%fused_computation.4 | convolution fusion | flops 1612185600 | bytes 2097152 | tf_op jit(solution)/shard_map/mrs,mst->mrt/dot_general | solution.py:18
  148.0 1.8 %fusion.16 = f32[512,512]{1,0:T(8,128)S(1)} fusion(f32[512,512]{1,0:T(8,128)S(1)} %fusion.13, f32[512,512]{1,0:T(8,128)S(1)} %fusion), kind=kOutput, calls=%fused_computation.27 | convolution fusion | flops 1610612736 | bytes 3145728 | tf_op jit(solution)/shard_map/mrs,mst->mrt/dot_general | solution.py:18
  149.8 4.3 %fusion.6 = bf16[512,512]{0,1:T(8,128)(2,1)} fusion(f32[512,512]{1,0:T(8,128)S(1)} %fusion.16, f32[1,512,512]{2,1,0:T(8,128)S(1)} %copy-done, f32[]{:T(128)S(6)} %div.12), kind=kOutput, calls=%fused_computation.13 | convolution fusion | flops 1611137024 | bytes 2621444 | tf_op jit(solution)/shard_map/mfr,mrs->mfs/dot_general | solution.py:50
  154.1 0.0 all-gather.3.cloned.1.call-update
  154.1 8.3 %all-gather.3.cloned.1.call-done = bf16[1024,512]{0,1:T(8,128)(2,1)} async-done(((bf16[512,512]{0,1:T(8,128)(2,1)}), bf16[1024,512]{0,1:T(8,128)(2,1)}) %all-gather.3.cloned.1.call-update) | async-done | bytes 1048592 | tf_op jit(solution)/shard_map/all_gather | solution.py:55
  162.4 2.3 %copy.3 = bf16[1024,512]{1,0:T(8,128)(2,1)} copy(bf16[1024,512]{0,1:T(8,128)(2,1)} %all-gather.3.cloned.1.call-done) | data formatting | bytes 2097152 | tf_op jit(solution)/shard_map/all_gather | solution.py:55
Async XLA Ops:
  6.5 1.2 copy-start
  6.5 121.3 %all-reduce.2.cloned.1.call-start = ((), (), s32[]{:S(2)}) async-start(), calls=%async_computation | async-start | bytes 2097152 | tf_op jit(solution)/shard_map/psum | solution.py:26
  10.6 151.8 %all-gather.3.cloned.1.call-start = ((), (), s32[]{:S(2)}) async-start(), calls=%async_computation.1 | async-start | bytes 1572864 | tf_op jit(solution)/shard_map/all_gather | solution.py:55
  127.8 2.7 %copy-start.1 = (f32[1,512,512]{2,1,0:T(8,128)S(1)}, f32[1,512,512]{2,1,0:T(8,128)}, u32[]{:S(2)}) copy-start(f32[1,512,512]{2,1,0:T(8,128)} %all-reduce.2.cloned.1.call-done) | copy-start | bytes 3145732
Sparse Core Ops, SparseCore 0:
  12.6 115.1 all-reduce.1
  154.2 8.0 all-gather.2
where the time goes:
time: 172 us; the launch traced here: 171 us
  waiting for transfers between devices  125 us (73%)
  matrix products  26.3 us (15%)
  between operations  14.2 us (8%)
  local copies, waits for them, and re-layouts  3.5 us (2%)
  other arithmetic  1.99 us (1%)
    psum x1, waiting for transfers between devices, reduce_gram(): return lax.psum(partial_gram, 'tensor')  117 us
    dot_general x9, matrix products, multiply(): jnp.einsum('mrs,mst->mrt', first_factor, second_factor, precision=lax.Pre...  19.2 us
    all_gather x1, waiting for transfers between devices, on_device(): return lax.all_gather(update, 'dp', axis=0, tiled=True)  8.26 us
    dot_general x1, matrix products, on_device(): jnp.einsum('mfr,mrs->mfs', gradient, replicated_total(gram_matrix), preci...  4.28 us
  transfers between devices with their start and end apart: 2, of which 2 were waited for; matrix products, arithmetic and copies ran while one was open for 0% of the time, Pallas kernels for 0%

commit v1 on v0

--- a/solution.py
+++ b/solution.py
@@ -3,6 +3,7 @@
 import jax.numpy as jnp
 from jax import lax
 from jax.sharding import PartitionSpec as P
+from jax.lax import all_gather
 
 FEATURES = 8192
 OUTPUTS = 512
@@ -14,6 +15,10 @@
 update_gain = 0.2
 
 
+def digits_register(buf):
+    return all_gather(buf, axis_name="tensor").sum(axis=0)
+
+
 def multiply(first_factor, second_factor):
     return jnp.einsum("mrs,mst->mrt", first_factor, second_factor, precision=lax.Precision.HIGHEST)
 
@@ -23,7 +28,7 @@
 
 
 def reduce_gram(partial_gram):
-    return lax.psum(partial_gram, "tensor")
+    return digits_register(partial_gram)
 
 
 def replicated_total(gram_matrix):

time: 172 us -> 254 us (1.48)
  waiting for transfers between devices: 125 us -> 201 us
  other arithmetic: 1.99 us -> 8.58 us
    all_gather x0 -> x1, waiting for transfers between devices: none -> 194 us  [digits_register(): return all_gather(buf, axis_name='tensor').sum(axis=0)]
    psum x1 -> x0, waiting for transfers between devices: 117 us -> none  [reduce_gram(): return lax.psum(partial_gram, 'tensor')]
    reduce_sum x0 -> x1, other arithmetic: none -> 7.91 us  [digits_register(): return all_gather(buf, axis_name='tensor').sum(axis=0)]
where the time goes in v1:
time: 254 us
  waiting for transfers between devices  201 us (79%)
  matrix products  26.3 us (10%)
  between operations  14.2 us (6%)
  other arithmetic  8.58 us (3%)
  local copies, waits for them, and re-layouts  3.5 us (1%)
    all_gather x1, waiting for transfers between devices, digits_register(): return all_gather(buf, axis_name='tensor').sum(axis=0)  194 us
    dot_general x9, matrix products, multiply(): jnp.einsum('mrs,mst->mrt', first_factor, second_factor, precision=lax.Pre...  19.2 us
    reduce_sum x1, other arithmetic, digits_register(): return all_gather(buf, axis_name='tensor').sum(axis=0)  7.91 us
    all_gather x1, waiting for transfers between devices, on_device(): return lax.all_gather(update, 'dp', axis=0, tiled=True)  7.37 us
  transfers between devices with their start and end apart: 2, of which 2 were waited for; matrix products, arithmetic and copies ran while one was open for 0% of the time, Pallas kernels for 0%

profile of v1, /device:TPU:0, one launch (start us, length us, event | category | flops | bytes accessed | tf_op | source)
XLA Modules:
  0.0 253.9 jit_solution(12230029904456417315)
XLA Ops:
  6.5 0.0 copy-start
  6.5 0.0 all-gather.5.cloned.1.call-start
  6.5 1.2 copy-done
  7.8 2.8 %fusion.6 = f32[512,512]{1,0:T(8,128)} fusion(f32[1,512,512]{2,1,0:T(8,128)S(1)} %copy-done), kind=kOutput, calls=%fused_computation.13 | convolution fusion | flops 1610612736 | bytes 2097152 | tf_op jit(solution)/shard_map/mfr,mfs->mrs/dot_general | solution.py:27
  10.6 0.0 all-gather.5.cloned.1.call-update
  10.6 0.0 all-gather.7.cloned.1.call-start
  10.7 193.8 %all-gather.5.cloned.1.call-done = f32[8192,512]{1,0:T(8,128)} async-done(((f32[512,512]{1,0:T(8,128)}), f32[8192,512]{1,0:T(8,128)}) %all-gather.5.cloned.1.call-update) | async-done | bytes 16777232 | tf_op jit(solution)/shard_map/all_gather | solution.py:19
  204.5 7.9 %reduce.2 = f32[512,512]{1,0:T(8,128)S(1)} reduce(f32[16,512,512]{2,1,0:T(8,128)} %bitcast.25, f32[]{:T(128)} %constant.7.clone.1), dimensions={0}, to_apply=%region_0.0 | reduce | flops 3932160 | bytes 17825796 | tf_op jit(solution)/shard_map/reduce_sum | solution.py:19
  212.4 0.7 select_reduce_fusion
  213.8 1.9 fusion.2
  215.7 1.9 fusion.8
  217.6 1.8 fusion.9
  219.5 1.9 fusion.1
  221.4 2.8 %fusion.11 = f32[512,512]{1,0:T(8,128)} fusion(f32[512,512]{1,0:T(8,128)S(1)} %fusion.1, f32[512,512]{1,0:T(8,128)S(1)} %fusion.9), kind=kOutput, calls=%fused_computation.21 | convolution fusion | flops 1610612736 | bytes 3145728 | tf_op jit(solution)/shard_map/mrs,mst->mrt/dot_general | solution.py:23
  224.2 2.0 fusion.10
  226.3 3.1 %fusion.12 = f32[512,512]{1,0:T(8,128)S(1)} fusion(f32[512,512]{1,0:T(8,128)} %fusion.11, f32[512,512]{1,0:T(8,128)S(1)} %fusion.1), kind=kOutput, calls=%fused_computation.22 | convolution fusion | flops 1610612736 | bytes 3145728 | tf_op jit(solution)/shard_map/mrs,mst->mrt/dot_general | solution.py:23
  229.3 1.9 fusion
  231.2 1.8 fusion.13
  233.1 4.3 %fusion.4 = bf16[512,512]{0,1:T(8,128)(2,1)} fusion(f32[512,512]{1,0:T(8,128)S(1)} %fusion.13, f32[1,512,512]{2,1,0:T(8,128)S(1)} %copy-done, f32[]{:T(128)S(6)} %div.23), kind=kOutput, calls=%fused_computation.11 | convolution fusion | flops 1611137024 | bytes 2621444 | tf_op jit(solution)/shard_map/mfr,mrs->mfs/dot_general | solution.py:55
  237.4 0.0 all-gather.7.cloned.1.call-update
  237.4 7.4 %all-gather.7.cloned.1.call-done = bf16[1024,512]{0,1:T(8,128)(2,1)} async-done(((bf16[512,512]{0,1:T(8,128)(2,1)}), bf16[1024,512]{0,1:T(8,128)(2,1)}) %all-gather.7.cloned.1.call-update) | async-done | bytes 1048592 | tf_op jit(solution)/shard_map/all_gather | solution.py:60
  244.8 2.3 copy.3
Async XLA Ops:
  6.5 1.2 copy-start
  6.5 198.0 %all-gather.5.cloned.1.call-start = ((), (), s32[]{:S(2)}) async-start(), calls=%async_computation | async-start | bytes 17825792 | tf_op jit(solution)/shard_map/all_gather | solution.py:19
  10.6 234.2 %all-gather.7.cloned.1.call-start = ((), (), s32[]{:S(2)}) async-start(), calls=%async_computation.1 | async-start | bytes 1572864 | tf_op jit(solution)/shard_map/all_gather | solution.py:60
Sparse Core Ops, SparseCore 0:
  10.7 193.7 all-gather.4
  237.5 7.2 all-gather.6
